TPU v7x, 32 devices: a whole 2x2x4 slice. The times are simulated.
32 devices in a mesh: rep: 4 (over z), fsdp: 2 (over x), tp: 4 (over y, core).
Axes of the slice: x: 2, y: 2, z: 4, core: 2. Of those that a mesh axis runs over, the one named last changes fastest.
Arguments:
- gate_pre: bfloat16 [1024, 14848], P(('rep', 'fsdp'), 'tp'), may hold values from -6 to 6
- up_pre: bfloat16 [1024, 14848], P(('rep', 'fsdp'), 'tp'), may hold values from -30 to 30
- out_grad: bfloat16 [1024, 4096], P(('rep', 'fsdp')), may hold values from -30 to 30
Outputs:
- down_grad: bfloat16 [4096, 14848], P('fsdp', 'tp')
All inputs are finite; a program needn't handle non-finite values.
Results may differ from a plain program's by a relative error of at most 0.02.
Values may be sent and summed in bfloat16 or wider, within the bound.
A program may use at most 128 MiB of HBM per device.

v0:
```python
import jax
import jax.numpy as jnp
from jax import lax
from jax.sharding import PartitionSpec as P


def on_device(gate_pre, up_pre, out_grad):
    hidden = (jax.nn.silu(gate_pre.astype(jnp.float32)) * up_pre.astype(jnp.float32)).astype(
        jnp.bfloat16
    )
    spread = lax.all_to_all(out_grad, "fsdp", split_axis=1, concat_axis=0, tiled=True)
    grad_rows = lax.all_gather(spread, "rep", axis=0, tiled=True)
    hidden_rows = lax.all_gather(hidden, ("rep", "fsdp"), axis=0, tiled=True)
    summed = lax.dot_general(
        grad_rows, hidden_rows, (((0,), (0,)), ((), ())), preferred_element_type=jnp.float32
    )
    square_total = lax.psum(jnp.sum(summed * summed), ("fsdp", "tp"))
    entry_count = summed.shape[0] * lax.axis_size("fsdp") * summed.shape[1] * lax.axis_size("tp")
    factor = 1.0 / jnp.sqrt(square_total / entry_count + 1e-06)
    return (summed * factor).astype(jnp.bfloat16)


def solution(mesh):
    return jax.shard_map(
        on_device,
        mesh=mesh,
        in_specs=(P(("rep", "fsdp"), "tp"), P(("rep", "fsdp"), "tp"), P(("rep", "fsdp"), None)),
        out_specs=P("fsdp", "tp"),
        check_vma=False,
    )
```

profile of v0, /device:TPU:0, one launch (start us, length us, event | category | flops | bytes accessed | tf_op | source)
XLA Modules:
  0.0 307.9 jit_solution(16072461343263493116)
XLA Ops:
  6.5 0.0 copy-start
  6.5 0.0 all-gather.5.cloned.1.call-start
  6.5 1.7 copy.6
  8.2 17.6 %all_to_all.19 = bf16[128,2,2048]{0,2,1:T(8,128)(2,1)S(1)} all-to-all(bf16[128,2,2048]{0,2,1:T(8,128)(2,1)S(1)} %bitcast.9), channel_id=1, replica_groups=mesh['rep'=4,'fsdp'=2,'tp'=4] {'fsdp'}, dimensions={1} | all-to-all | bytes 2097152 | tf_op jit(solution)/shard_map/all_to_all | solution.py:11
  25.9 1.3 copy.7
  27.2 0.0 all-gather.5.cloned.1.call-update
  27.2 0.0 all-gather.3.cloned.1.call-start
  27.2 0.0 copy-done
  27.3 2.7 fusion.5
  30.0 0.0 all-gather.3.cloned.1.call-update
  30.0 78.6 %all-gather.5.cloned.1.call-done = bf16[1024,2048]{1,0:T(8,128)(2,1)} async-done(((bf16[256,2048]{1,0:T(8,128)(2,1)}), bf16[1024,2048]{1,0:T(8,128)(2,1)}) %all-gather.5.cloned.1.call-update) | async-done | bytes 4194320 | tf_op jit(solution)/shard_map/all_gather | solution.py:12
  108.6 115.4 %all-gather.3.cloned.1.call-done = bf16[1024,3712]{1,0:T(8,128)(2,1)} async-done(((bf16[128,3712]{1,0:T(8,128)(2,1)}), bf16[1024,3712]{1,0:T(8,128)(2,1)}) %all-gather.3.cloned.1.call-update) | async-done | bytes 7602192 | tf_op jit(solution)/shard_map/all_gather | solution.py:13
  224.0 28.3 %multiply_reduce_fusion = (f32[]{:T(128)}, f32[3712,2048]{1,0:T(8,128)}) fusion(bf16[1024,3712]{1,0:T(8,128)(2,1)} %all-gather.3.cloned.1.call-done, bf16[1024,2048]{1,0:T(8,128)(2,1)} %all-gather.5.cloned.1.call-done), kind=kOutput, calls=%fused_computation.1 | convolution fusion | flops 15584460800 | bytes 42205188 | tf_op jit(solution)/shard_map/dot_general | solution.py:14
  252.3 12.4 %psum.7 = f32[]{:T(128)} all-reduce(f32[]{:T(128)} %get-tuple-element.5), channel_id=1, replica_groups=mesh['rep'=4,'fsdp'=2,'tp'=4] {'fsdp','tp'}, use_global_device_ids=true, to_apply=%region_1.2 | all-reduce | flops 1 | bytes 8 | tf_op jit(solution)/shard_map/psum | solution.py:17
  265.4 16.7 %fusion = bf16[2048,3712]{0,1:T(8,128)(2,1)} fusion(f32[3712,2048]{1,0:T(8,128)} %get-tuple-element.6, f32[]{:T(128)S(6)} %sqrt.3), kind=kLoop, calls=%fused_computation.2 | loop fusion | flops 15204352 | bytes 45613060 | tf_op jit(solution)/shard_map/convert_element_type | solution.py:20
  282.1 19.0 %copy.8 = bf16[2048,3712]{1,0:T(8,128)(2,1)} copy(bf16[2048,3712]{0,1:T(8,128)(2,1)} %fusion) | data formatting | bytes 30408704 | tf_op jit(solution)/shard_map/convert_element_type | solution.py:20
Async XLA Ops:
  6.5 20.7 %copy-start = (bf16[128,3712]{1,0:T(8,128)(2,1)S(1)}, bf16[128,3712]{1,0:T(8,128)(2,1)}, u32[]{:S(2)}) copy-start(bf16[128,3712]{1,0:T(8,128)(2,1)} %param.4) | copy-start | bytes 2850820
  6.5 102.1 %all-gather.5.cloned.1.call-start = ((), (), s32[]{:S(2)}) async-start(), calls=%async_computation.2 | async-start | bytes 5242880 | tf_op jit(solution)/shard_map/all_gather | solution.py:12
  27.2 196.8 %all-gather.3.cloned.1.call-start = ((), (), s32[]{:S(2)}) async-start(), calls=%async_computation.1 | async-start | bytes 8552448 | tf_op jit(solution)/shard_map/all_gather | solution.py:13
Sparse Core Ops, SparseCore 0:
  27.3 81.2 all-gather.4
  110.8 113.1 all-gather.2
where the time goes:
time: 309 us; the launch traced here: 308 us
  waiting for transfers between devices  194 us (63%)
  blocking collectives  30.1 us (10%)
  matrix products  28.3 us (9%)
  local copies, waits for them, and re-layouts  22 us (7%)
  other arithmetic  19.4 us (6%)
  between operations  14.1 us (5%)
    all_gather x1, waiting for transfers between devices, on_device(): hidden_rows = lax.all_gather(hidden, ('rep', 'fsdp'), axis=0, tiled=True)  115 us
    all_gather x1, waiting for transfers between devices, on_device(): grad_rows = lax.all_gather(spread, 'rep', axis=0, tiled=True)  78.6 us
    dot_general x1, matrix products, on_device(): lax.dot_general(grad_rows, hidden_rows, (((0,), (0,)), ((), ())), preferr...  28.3 us
    convert_element_type x1, local copies, waits for them, and re-layouts, on_device(): return (summed * factor).astype(jnp.bfloat16)  19 us
    all_to_all x1, blocking collectives, on_device(): lax.all_to_all(out_grad, 'fsdp', split_axis=1, concat_axis=0, tiled=True)  17.6 us
    convert_element_type x1, other arithmetic, on_device(): return (summed * factor).astype(jnp.bfloat16)  16.7 us
    psum x1, blocking collectives, on_device(): square_total = lax.psum(jnp.sum(summed * summed), ('fsdp', 'tp'))  12.4 us
  transfers between devices with their start and end apart: 2, of which 2 were waited for; matrix products, arithmetic and copies ran while one was open for 1% of the time, Pallas kernels for 0%

commit v1 on v0

--- a/solution.py
+++ b/solution.py
@@ -8,7 +8,10 @@
     hidden = (jax.nn.silu(gate_pre.astype(jnp.float32)) * up_pre.astype(jnp.float32)).astype(
         jnp.bfloat16
     )
-    spread = lax.all_to_all(out_grad, "fsdp", split_axis=1, concat_axis=0, tiled=True)
+    size = lax.axis_size("fsdp")
+    shards = jnp.stack(jnp.split(out_grad, size, axis=1), axis=0)
+    shards = lax.all_to_all(shards, "fsdp", split_axis=0, concat_axis=0)
+    spread = jnp.concatenate(shards, axis=0)
     grad_rows = lax.all_gather(spread, "rep", axis=0, tiled=True)
     hidden_rows = lax.all_gather(hidden, ("rep", "fsdp"), axis=0, tiled=True)
     summed = lax.dot_general(

time: 309 us -> 287 us (0.929)
  local copies, waits for them, and re-layouts: 22 us -> 1.41 us
    convert_element_type x1 -> x0, local copies, waits for them, and re-layouts: 19 us -> none  [on_device(): return (summed * factor).astype(jnp.bfloat16)]
where the time goes in v1:
time: 287 us
  waiting for transfers between devices  195 us (68%)
  blocking collectives  30.8 us (11%)
  matrix products  27.6 us (10%)
  other arithmetic  17.6 us (6%)
  between operations  14.1 us (5%)
    all_gather x1, waiting for transfers between devices, on_device(): hidden_rows = lax.all_gather(hidden, ('rep', 'fsdp'), axis=0, tiled=True)  115 us
    all_gather x1, waiting for transfers between devices, on_device(): grad_rows = lax.all_gather(spread, 'rep', axis=0, tiled=True)  79.9 us
    dot_general x1, matrix products, on_device(): lax.dot_general(grad_rows, hidden_rows, (((0,), (0,)), ((), ())), preferr...  27.6 us
    all_to_all x1, blocking collectives, on_device(): shards = lax.all_to_all(shards, 'fsdp', split_axis=0, concat_axis=0)  18.3 us
    convert_element_type x1, other arithmetic, on_device(): return (summed * factor).astype(jnp.bfloat16)  16 us
    psum x1, blocking collectives, on_device(): square_total = lax.psum(jnp.sum(summed * summed), ('fsdp', 'tp'))  12.4 us
  transfers between devices with their start and end apart: 2, of which 2 were waited for; matrix products, arithmetic and copies ran while one was open for 1% of the time, Pallas kernels for 0%

profile of v1, /device:TPU:0, one launch (start us, length us, event | category | flops | bytes accessed | tf_op | source)
XLA Modules:
  0.0 286.9 jit_solution(17649946681174013479)
XLA Ops:
  6.5 0.0 copy-start
  6.5 0.0 copy-start.1
  6.5 0.0 all-gather.3.cloned.1.call-start
  6.5 1.4 slice_bitcast_fusion.1
  7.9 0.1 pad_maximum_fusion
  8.1 18.3 %all_to_all.5 = bf16[2,128,2048]{2,1,0:T(8,128)(2,1)} all-to-all(bf16[2,128,2048]{2,1,0:T(8,128)(2,1)S(1)} %pad_maximum_fusion), channel_id=1, replica_groups=mesh['rep'=4,'fsdp'=2,'tp'=4] {'fsdp'}, dimensions={0} | all-to-all | bytes 2097152 | tf_op jit(solution)/shard_map/all_to_all | solution.py:13
  26.4 0.0 all-gather.3.cloned.1.call-update
  26.4 0.0 all-gather.5.cloned.1.call-start
  26.5 0.0 copy-done
  26.5 0.0 copy-done.1
  26.5 1.5 fusion.4
  28.0 0.0 all-gather.5.cloned.1.call-update
  28.0 79.9 %all-gather.3.cloned.1.call-done = bf16[1024,2048]{1,0:T(8,128)(2,1)} async-done(((bf16[256,2048]{1,0:T(8,128)(2,1)}), bf16[1024,2048]{1,0:T(8,128)(2,1)}) %all-gather.3.cloned.1.call-update) | async-done | bytes 4194320 | tf_op jit(solution)/shard_map/all_gather | solution.py:15
  107.9 115.4 %all-gather.5.cloned.1.call-done = bf16[1024,3712]{1,0:T(8,128)(2,1)} async-done(((bf16[128,3712]{1,0:T(8,128)(2,1)}), bf16[1024,3712]{1,0:T(8,128)(2,1)}) %all-gather.5.cloned.1.call-update) | async-done | bytes 7602192 | tf_op jit(solution)/shard_map/all_gather | solution.py:16
  223.3 27.6 %multiply_reduce_fusion = (f32[]{:T(128)}, f32[2048,3712]{1,0:T(8,128)}) fusion(bf16[1024,2048]{1,0:T(8,128)(2,1)} %all-gather.3.cloned.1.call-done, bf16[1024,3712]{1,0:T(8,128)(2,1)} %all-gather.5.cloned.1.call-done), kind=kOutput, calls=%fused_computation.1 | convolution fusion | flops 15584460800 | bytes 42205188 | tf_op jit(solution)/shard_map/dot_general | solution.py:17
  250.9 12.4 %psum.7 = f32[]{:T(128)} all-reduce(f32[]{:T(128)} %get-tuple-element.7), channel_id=1, replica_groups=mesh['rep'=4,'fsdp'=2,'tp'=4] {'fsdp','tp'}, use_global_device_ids=true, to_apply=%region_1.2 | all-reduce | flops 1 | bytes 8 | tf_op jit(solution)/shard_map/psum | solution.py:20
  264.0 16.0 %multiply_convert_fusion = bf16[2048,3712]{1,0:T(8,128)(2,1)} fusion(f32[2048,3712]{1,0:T(8,128)} %get-tuple-element.8, f32[]{:T(128)S(6)} %sqrt.3), kind=kLoop, calls=%fused_computation | loop fusion | flops 15204352 | bytes 45613060 | tf_op jit(solution)/shard_map/convert_element_type | solution.py:23
Async XLA Ops:
  6.5 19.9 %copy-start = (bf16[128,3712]{1,0:T(8,128)(2,1)S(1)}, bf16[128,3712]{1,0:T(8,128)(2,1)}, u32[]{:S(2)}) copy-start(bf16[128,3712]{1,0:T(8,128)(2,1)} %param.4) | copy-start | bytes 2850820
  6.5 19.9 %copy-start.1 = (bf16[128,3712]{1,0:T(8,128)(2,1)S(1)}, bf16[128,3712]{1,0:T(8,128)(2,1)}, u32[]{:S(2)}) copy-start(bf16[128,3712]{1,0:T(8,128)(2,1)} %param.3) | copy-start | bytes 2850820
  6.5 101.3 %all-gather.3.cloned.1.call-start = ((), (), s32[]{:S(2)}) async-start(), calls=%async_computation.1 | async-start | bytes 5242880 | tf_op jit(solution)/shard_map/all_gather | solution.py:15
  26.4 196.9 %all-gather.5.cloned.1.call-start = ((), (), s32[]{:S(2)}) async-start(), calls=%async_computation.2 | async-start | bytes 8552448 | tf_op jit(solution)/shard_map/all_gather | solution.py:16
Sparse Core Ops, SparseCore 0:
  26.5 81.2 all-gather.2
  110.1 113.1 all-gather.4

commit v2 on v0

--- a/solution.py
+++ b/solution.py
@@ -9,7 +9,19 @@
         jnp.bfloat16
     )
     spread = lax.all_to_all(out_grad, "fsdp", split_axis=1, concat_axis=0, tiled=True)
-    grad_rows = lax.all_gather(spread, "rep", axis=0, tiled=True)
+    tray = [spread]
+    c = 0
+    many = jax.lax.psum(1, axis_name="rep")
+    while c < many - 1:
+        tray.append(
+            jax.lax.ppermute(
+                tray[-1], "rep", perm=[(hop_no, (hop_no + 1) % many) for hop_no in range(many)]
+            )
+        )
+        c = c + 1
+    grad_rows = jnp.roll(
+        jnp.concatenate(tray[::-1], 0), (jax.lax.axis_index("rep") + 1) * spread.shape[0], 0
+    )
     hidden_rows = lax.all_gather(hidden, ("rep", "fsdp"), axis=0, tiled=True)
     summed = lax.dot_general(
         grad_rows, hidden_rows, (((0,), (0,)), ((), ())), preferred_element_type=jnp.float32

time: 309 us -> 263 us (0.85)
  waiting for transfers between devices: 194 us -> 135 us
  starting transfers between devices: 0.04 us -> 17.6 us
  local copies, waits for them, and re-layouts: 22 us -> 13 us
  blocking collectives: 30.1 us -> 36.8 us
    ppermute x0 -> x3, waiting for transfers between devices: none -> 135 us  [on_device(): jax.lax.ppermute(tray[-1], 'rep', perm=[(hop_no, (hop_no + 1) % many) for...]
    all_gather x1, waiting for transfers between devices: 115 us -> 0.01 us  [on_device(): hidden_rows = lax.all_gather(hidden, ('rep', 'fsdp'), axis=0, tiled=True)]
    all_gather x1 -> x0, waiting for transfers between devices: 78.6 us -> none  [on_device(): grad_rows = lax.all_gather(spread, 'rep', axis=0, tiled=True)]
    convert_element_type x1 -> x0, local copies, waits for them, and re-layouts: 19 us -> none  [on_device(): return (summed * factor).astype(jnp.bfloat16)]
    ppermute x0 -> x3, starting transfers between devices: none -> 17.6 us  [on_device(): jax.lax.ppermute(tray[-1], 'rep', perm=[(hop_no, (hop_no + 1) % many) for...]
    unnamed x3 -> x8, local copies, waits for them, and re-layouts: 1.7 us -> 11.4 us
    all_to_all x1, blocking collectives: 17.6 us -> 24.4 us  [on_device(): lax.all_to_all(out_grad, 'fsdp', split_axis=1, concat_axis=0, tiled=True)]
  transfers between devices with their start and end apart: 2 -> 4, of which waited for: 2 -> 3; matrix products, arithmetic and copies ran while one was open for 1% -> 5% of each run, Pallas kernels for 0% -> 0%
where the time goes in v2:
time: 263 us
  waiting for transfers between devices  135 us (51%)
  blocking collectives  36.8 us (14%)
  matrix products  27.6 us (10%)
  other arithmetic  19.1 us (7%)
  starting transfers between devices  17.6 us (7%)
  between operations  14.1 us (5%)
  local copies, waits for them, and re-layouts  13 us (5%)
    ppermute x3, waiting for transfers between devices, on_device(): jax.lax.ppermute(tray[-1], 'rep', perm=[(hop_no, (hop_no + 1) % many) for...  135 us
    dot_general x1, matrix products, on_device(): lax.dot_general(grad_rows, hidden_rows, (((0,), (0,)), ((), ())), preferr...  27.6 us
    all_to_all x1, blocking collectives, on_device(): lax.all_to_all(out_grad, 'fsdp', split_axis=1, concat_axis=0, tiled=True)  24.4 us
    ppermute x3, starting transfers between devices, on_device(): jax.lax.ppermute(tray[-1], 'rep', perm=[(hop_no, (hop_no + 1) % many) for...  17.6 us
    convert_element_type x1, other arithmetic, on_device(): return (summed * factor).astype(jnp.bfloat16)  16 us
    psum x1, blocking collectives, on_device(): square_total = lax.psum(jnp.sum(summed * summed), ('fsdp', 'tp'))  12.4 us
    unnamed x8, local copies, waits for them, and re-layouts  11.4 us
  transfers between devices with their start and end apart: 4, of which 3 were waited for; matrix products, arithmetic and copies ran while one was open for 5% of the time, Pallas kernels for 0%

profile of v2, /device:TPU:0, one launch (start us, length us, event | category | flops | bytes accessed | tf_op | source)
XLA Modules:
  0.0 262.8 jit_solution(4408487592586069644)
XLA Ops:
  6.5 0.0 all-gather.2.cloned.1.call-start
  6.5 3.0 %fusion.6 = bf16[128,3712]{1,0:T(8,128)(2,1)} fusion(bf16[128,3712]{1,0:T(8,128)(2,1)} %param.4, bf16[128,3712]{1,0:T(8,128)(2,1)} %param.3), kind=kLoop, calls=%fused_computation.10 | loop fusion | flops 3801088 | bytes 2850816 | tf_op jit(solution)/shard_map/convert_element_type | solution.py:8
  9.6 0.0 all-gather.2.cloned.1.call-update
  9.6 1.6 copy.4
  11.2 24.4 %all_to_all.19 = bf16[128,2,2048]{0,2,1:T(8,128)(2,1)S(1)} all-to-all(bf16[128,2,2048]{0,2,1:T(8,128)(2,1)S(1)} %bitcast.8), channel_id=1, replica_groups=mesh['rep'=4,'fsdp'=2,'tp'=4] {'fsdp'}, dimensions={1} | all-to-all | bytes 2097152 | tf_op jit(solution)/shard_map/all_to_all | solution.py:11
  35.7 0.5 copy.5
  36.2 1.9 collective-permute-start
  38.1 40.7 %collective-permute-done = bf16[256,2048]{1,0:T(8,128)(2,1)S(1)} collective-permute-done((bf16[256,2048]{1,0:T(8,128)(2,1)S(1)}, bf16[256,2048]{1,0:T(8,128)(2,1)S(1)}, u32[]{:S(2)}, u32[]{:S(2)}) %collective-permute-start) | collective-permute-done | bytes 1048608 | tf_op jit(solution)/shard_map/ppermute | solution.py:17
  78.8 0.0 collective-permute-start.1
  78.8 49.1 %collective-permute-done.1 = bf16[256,2048]{1,0:T(8,128)(2,1)S(1)} collective-permute-done((bf16[256,2048]{1,0:T(8,128)(2,1)S(1)}, bf16[256,2048]{1,0:T(8,128)(2,1)S(1)}, u32[]{:S(2)}, u32[]{:S(2)}) %collective-permute-start.1) | collective-permute-done | bytes 1048608 | tf_op jit(solution)/shard_map/ppermute | solution.py:17
  127.9 15.7 %collective-permute-start.2 = (bf16[256,2048]{1,0:T(8,128)(2,1)S(1)}, bf16[256,2048]{1,0:T(8,128)(2,1)}, u32[]{:S(2)}, u32[]{:S(2)}) collective-permute-start(bf16[256,2048]{1,0:T(8,128)(2,1)S(1)} %collective-permute-done.1), channel_id=1, source_target_pairs={{0,8},{8,16},{16,24},{24,0},{1,9},{9,17},{17,25},{25,1},{2,10},{10... | collective-permute-start | bytes 3145736 | tf_op jit(solution)/shard_map/ppermute | solution.py:17
  143.6 44.7 %collective-permute-done.2 = bf16[256,2048]{1,0:T(8,128)(2,1)} collective-permute-done((bf16[256,2048]{1,0:T(8,128)(2,1)S(1)}, bf16[256,2048]{1,0:T(8,128)(2,1)}, u32[]{:S(2)}, u32[]{:S(2)}) %collective-permute-start.2) | collective-permute-done | bytes 1048608 | tf_op jit(solution)/shard_map/ppermute | solution.py:17
  188.3 2.3 constant_dynamic-update-slice_fusion.7
  190.6 1.0 constant_dynamic-update-slice_fusion.6
  191.7 1.0 constant_dynamic-update-slice_fusion.5
  192.7 1.0 constant_dynamic-update-slice_fusion.4
  193.8 2.3 constant_dynamic-update-slice_fusion.3
  196.1 1.0 constant_dynamic-update-slice_fusion.2
  197.1 1.0 constant_dynamic-update-slice_fusion.1
  198.1 1.0 constant_dynamic-update-slice_fusion
  199.2 0.0 all-gather.2.cloned.1.call-done
  199.2 27.6 %multiply_reduce_fusion = (f32[]{:T(128)}, f32[2048,3712]{1,0:T(8,128)}) fusion(bf16[1024,3712]{1,0:T(8,128)(2,1)} %all-gather.2.cloned.1.call-done, bf16[2048,2048]{1,0:T(8,128)(2,1)} %constant_dynamic-update-slice_fusion, s32[]{:T(128)S(6)} %select_n.14), kind=kOutput, calls=%fused_computation.1 | convolution fusion | flops 15584460800 | bytes 42205192 | tf_op jit(solution)/shard_map/dot_general | solution.py:26
  226.8 12.4 %psum.7 = f32[]{:T(128)} all-reduce(f32[]{:T(128)} %get-tuple-element.5), channel_id=1, replica_groups=mesh['rep'=4,'fsdp'=2,'tp'=4] {'fsdp','tp'}, use_global_device_ids=true, to_apply=%region_1.2 | all-reduce | flops 1 | bytes 8 | tf_op jit(solution)/shard_map/psum | solution.py:29
  239.9 16.0 %multiply_convert_fusion = bf16[2048,3712]{1,0:T(8,128)(2,1)} fusion(f32[2048,3712]{1,0:T(8,128)} %get-tuple-element.6, f32[]{:T(128)S(6)} %sqrt.3), kind=kLoop, calls=%fused_computation | loop fusion | flops 15204352 | bytes 45613060 | tf_op jit(solution)/shard_map/convert_element_type | solution.py:32
Async XLA Ops:
  6.5 192.6 %all-gather.2.cloned.1.call-start = ((), (), s32[]{:S(2)}) async-start(), calls=%async_computation.1 | async-start | bytes 8552448 | tf_op jit(solution)/shard_map/all_gather | solution.py:25
  36.2 42.6 %collective-permute-start = (bf16[256,2048]{1,0:T(8,128)(2,1)S(1)}, bf16[256,2048]{1,0:T(8,128)(2,1)S(1)}, u32[]{:S(2)}, u32[]{:S(2)}) collective-permute-start(bf16[256,2048]{1,0:T(8,128)(2,1)S(1)} %bitcast.4), channel_id=1, source_target_pairs={{0,8},{8,16},{16,24},{24,0},{1,9},{9,17},{17,25},{25,1},{2,10},{10... | collective-permute-start | bytes 3145736 | tf_op jit(solution)/shard_map/ppermute | solution.py:17
  78.8 49.1 %collective-permute-start.1 = (bf16[256,2048]{1,0:T(8,128)(2,1)S(1)}, bf16[256,2048]{1,0:T(8,128)(2,1)S(1)}, u32[]{:S(2)}, u32[]{:S(2)}) collective-permute-start(bf16[256,2048]{1,0:T(8,128)(2,1)S(1)} %collective-permute-done), channel_id=1, source_target_pairs={{0,8},{8,16},{16,24},{24,0},{1,9},{9,17},{17,25},{25,1},{2,10},{10... | collective-permute-start | bytes 3145736 | tf_op jit(solution)/shard_map/ppermute | solution.py:17
  127.9 60.4 %collective-permute-start.2 = (bf16[256,2048]{1,0:T(8,128)(2,1)S(1)}, bf16[256,2048]{1,0:T(8,128)(2,1)}, u32[]{:S(2)}, u32[]{:S(2)}) collective-permute-start(bf16[256,2048]{1,0:T(8,128)(2,1)S(1)} %collective-permute-done.1), channel_id=1, source_target_pairs={{0,8},{8,16},{16,24},{24,0},{1,9},{9,17},{17,25},{25,1},{2,10},{10... | collective-permute-start | bytes 3145736 | tf_op jit(solution)/shard_map/ppermute | solution.py:17
Sparse Core Ops, SparseCore 0:
  9.7 175.5 all-gather.1
